TPU v7x, 256 devices: a 2x2x32 block of a 4x8x32 slice. The times are simulated.
256 devices in a mesh: rep: 4 (over y, x), section: 2 (over core), wide: 32 (over z).
Axes of the slice: x: 2, y: 2, z: 32, core: 2. Of those that a mesh axis runs over, the one named last changes fastest.
The devices are a block of a 4x8x32 slice.
Arguments:
- acts: bfloat16 [2, 1024, 8192], P('section', 'rep', 'wide'), parts along dimension 1, may hold values from -100 to 100
- norm_gain: bfloat16 [2, 8192], P('section', 'wide'), may hold values from 0.099609375 to 1.8984375
- w_qkv: bfloat16 [2, 8192, 5120], P('section', None, 'wide'), may hold values from -0.0625 to 0.0625
- w_out: bfloat16 [2, 4096, 8192], P('section', None, 'wide'), may hold values from -0.5 to 0.5
- key_cache: bfloat16 [2, 1024, 384, 512], P('section', ('rep', 'wide')), parts along dimension 1, may hold values from -400 to 400
- value_cache: bfloat16 [2, 1024, 384, 512], P('section', ('rep', 'wide')), parts along dimension 1, may hold values from -6 to 6
- cache_lengths: int32 [2, 1024], P('section', ('rep', 'wide')), parts along dimension 1, may hold values from 2 to 384, as said below
- slot_of: int32 [2, 1024], P('section', 'rep'), parts along dimension 1, may hold values from 0 to 255, each once within a row
Outputs:
- handed: bfloat16 [2, 1024, 8192], P('section', 'rep', 'wide'), parts along dimension 1
There are 4 independent parts, one for each index of `rep`. A program takes and returns all parts, laid end to end along the dimension named above; an argument that names none is the same for every part. Nothing has to cross between parts.
Inputs may be any that keep to these rules, and one draw needn't show every extreme that they name: `cache_lengths`: slot j of a section belongs to owner j // 8; in every section some slot holds exactly 384. `slot_of`: each section's row names every slot once.
All inputs are finite; a program needn't handle non-finite values.
Results may differ from a plain program's by a relative error of at most 0.005.
Values may be sent and summed in bfloat16 or wider, within the bound.
No kernel may reach another device: no remote copies, remote signals or barrier semaphores. Data moves between devices by JAX's collectives and lax.ppermute only.
A program may use at most 64 MiB of HBM per device.

v0:
```python
import math
import jax
import jax.numpy as jnp
from jax import lax
from jax.sharding import PartitionSpec as P

D = 8192
HEADS = 32
KV_HEADS = 4
HDIM = 128
epsilon = 1e-05
rope_base = 500000.0
masked_score = -1e30


def copy_for_each(value, axis):
    count = lax.axis_size(axis)
    return lax.all_to_all(
        jnp.broadcast_to(value[None], (count, *value.shape)), axis, 0, 0, tiled=True
    )


def of_everyone(value, axis):
    return copy_for_each(value, axis).sum(axis=0)


def passed_along(value, axis, steps):
    count = lax.axis_size(axis)
    pairs = [(source, (source + steps) % count) for source in range(count)]
    return lax.ppermute(value, axis, pairs)


def rotate(values, position):
    half_dim = HDIM // 2
    exponent = jnp.arange(half_dim, dtype=jnp.float32) * (2.0 / HDIM)
    frequency = jnp.exp(-math.log(rope_base) * exponent)
    angle = position[..., None] * frequency
    cosine = jnp.cos(angle)
    sine = jnp.sin(angle)
    first_half = values[..., :half_dim]
    second_half = values[..., half_dim:]
    return jnp.concatenate(
        [first_half * cosine - second_half * sine, second_half * cosine + first_half * sine],
        axis=-1,
    )


def attend(joined_rows, key_rows, value_rows, lengths_here):
    row_count = joined_rows.shape[0]
    groups = HEADS // KV_HEADS
    query_width = HEADS * HDIM
    kv_width = KV_HEADS * HDIM
    queries = joined_rows[:, :query_width].reshape(row_count, KV_HEADS, groups, HDIM)
    new_keys = joined_rows[:, query_width : query_width + kv_width].reshape(
        row_count, KV_HEADS, HDIM
    )
    new_values = joined_rows[:, query_width + kv_width :].reshape(row_count, KV_HEADS, HDIM)
    position = lengths_here.astype(jnp.float32)
    queries = rotate(queries.astype(jnp.float32), position[:, None, None]).astype(jnp.bfloat16)
    new_keys = rotate(new_keys.astype(jnp.float32), position[:, None]).astype(jnp.bfloat16)
    score_scale = 1.0 / math.sqrt(HDIM)
    cache_span = key_rows.shape[1]
    cached_keys = key_rows.reshape(row_count, cache_span, KV_HEADS, HDIM)
    cached_values = value_rows.reshape(row_count, cache_span, KV_HEADS, HDIM)
    own_score = (
        jnp.einsum("ngqd,ngd->ngq", queries, new_keys, preferred_element_type=jnp.float32)
        * score_scale
    )
    scores = (
        jnp.einsum("ngqd,nlgd->ngql", queries, cached_keys, preferred_element_type=jnp.float32)
        * score_scale
    )
    live_mask = (jnp.arange(cache_span, dtype=jnp.int32)[None, :] < lengths_here[:, None])[
        :, None, None, :
    ]
    masked = jnp.where(live_mask, scores, masked_score)
    peak = jnp.maximum(jnp.max(masked, axis=-1), own_score)
    weights = jnp.where(live_mask, jnp.exp(masked - peak[..., None]), 0.0)
    sums = jnp.sum(weights, axis=-1)
    weighted = jnp.einsum(
        "ngql,nlgd->ngqd",
        weights.astype(jnp.bfloat16),
        cached_values,
        preferred_element_type=jnp.float32,
    )
    own_weight = jnp.exp(own_score - peak)
    denominator = sums + own_weight
    own_rounded = own_weight.astype(jnp.bfloat16).astype(jnp.float32)
    weighted = weighted + own_rounded[..., None] * new_values.astype(jnp.float32)[:, :, None, :]
    return (weighted / denominator[..., None]).reshape(row_count, query_width).astype(jnp.bfloat16)


def shards(acts, norm_gain, w_qkv, w_out, key_cache, value_cache, cache_lengths, slot_of):
    tokens = acts[0].astype(jnp.float32)
    squares = of_everyone(jnp.sum(tokens * tokens, axis=1), "wide")
    normed = (
        tokens * lax.rsqrt(squares / D + epsilon)[:, None] * norm_gain[0].astype(jnp.float32)
    ).astype(jnp.bfloat16)
    slot_table = slot_of[0]
    request_total = slot_table.shape[0]
    request_at_slot = (
        jnp.zeros((request_total,), jnp.int32)
        .at[slot_table]
        .set(jnp.arange(request_total, dtype=jnp.int32))
    )
    projection = w_qkv[0]
    whole = lax.all_gather(normed, "wide", axis=1, tiled=True)
    columns = jnp.dot(whole, projection, preferred_element_type=jnp.float32).astype(jnp.bfloat16)
    joined_rows = lax.all_to_all(
        columns[request_at_slot], "wide", split_axis=0, concat_axis=1, tiled=True
    )
    attended = attend(joined_rows, key_cache[0], value_cache[0], cache_lengths[0])
    out_weight = w_out[0]
    projected = jnp.dot(
        lax.all_gather(attended, "wide", axis=0, tiled=True),
        out_weight,
        preferred_element_type=jnp.float32,
    )
    updated = (tokens + projected[slot_table]).astype(jnp.bfloat16)
    return passed_along(updated[None], "section", 1)


def solution(mesh):
    placed = (
        P("section", "rep", "wide"),
        P("section", "wide"),
        P("section", None, "wide"),
        P("section", None, "wide"),
        P("section", ("rep", "wide"), None, None),
        P("section", ("rep", "wide"), None, None),
        P("section", ("rep", "wide")),
        P("section", "rep"),
    )
    return jax.shard_map(
        shards, mesh=mesh, in_specs=placed, out_specs=P("section", "rep", "wide"), check_vma=False
    )
```

profile of v0, /device:TPU:37, one launch (start us, length us, event | category | flops | bytes accessed | tf_op | source)
XLA Modules:
  0.0 379.6 jit_solution(14781178704558300775)
XLA Ops:
  6.5 0.0 copy-start
  6.6 1.2 fusion.33
  7.7 0.6 broadcast_in_dim.23
  8.4 33.2 %all-to-all-start = ((f32[32,1,256]{2,1,0:T(1,128)}), f32[32,1,256]{2,1,0:T(1,128)S(1)}, u32[]{:S(2)}, u32[]{:S(2)}) async-start(f32[32,1,256]{2,1,0:T(1,128)} %broadcast_in_dim.23), calls=%async_computation | async-start | bytes 65536 | tf_op jit(solution)/shard_map/all_to_all | solution.py:18
  41.6 0.1 all-gather.3.cloned.1.call-start
  41.6 0.7 mul.188
  42.3 20.6 %all-to-all-done = f32[32,1,256]{2,1,0:T(1,128)S(1)} async-done(((f32[32,1,256]{2,1,0:T(1,128)}), f32[32,1,256]{2,1,0:T(1,128)S(1)}, u32[]{:S(2)}, u32[]{:S(2)}) %all-to-all-start) | async-done | bytes 32800 | tf_op jit(solution)/shard_map/all_to_all | solution.py:18
  63.0 0.1 reduce_sum.28
  63.0 1.7 fusion.35
  64.7 0.1 all-gather.3.cloned.1.call-update
  64.8 5.5 %reshape_squeeze.6 = bf16[8,384,4,128]{3,2,1,0:T(4,128)(2,1)} reshape(bf16[1,8,384,512]{3,2,1,0:T(8,128)(2,1)} %param.12) | data formatting | bytes 6291456 | tf_op jit(solution)/shard_map/reshape;squeeze | solution.py:63
  70.3 0.0 copy-start.3
  70.3 5.5 %reshape_squeeze.7 = bf16[8,384,4,128]{3,2,1,0:T(4,128)(2,1)} reshape(bf16[1,8,384,512]{3,2,1,0:T(8,128)(2,1)} %param.13) | data formatting | bytes 6291456 | tf_op jit(solution)/shard_map/reshape;squeeze | solution.py:64
  75.8 0.0 copy-done.3
  75.8 1.4 scatter_custom_fusion
  77.3 0.0 copy-start.4
  77.3 100.0 %all-gather.3.cloned.1.call-done = bf16[256,8192]{1,0:T(8,128)(2,1)} async-done(((bf16[256,256]{1,0:T(8,128)(2,1)}), bf16[256,8192]{1,0:T(8,128)(2,1)}) %all-gather.3.cloned.1.call-update) | async-done | bytes 4194320 | tf_op jit(solution)/shard_map/all_gather | solution.py:107
  177.3 0.0 copy-done
  177.3 3.7 fusion.20
  181.0 0.1 copy.25
  181.1 1.8 gather_fusion
  183.0 12.1 %all-to-all-start.1 = ((bf16[32,8,160]{2,1,0:T(8,128)(2,1)}), bf16[32,8,160]{2,1,0:T(8,128)(2,1)S(1)}, u32[]{:S(2)}, u32[]{:S(2)}) async-start(bf16[32,8,160]{2,1,0:T(8,128)(2,1)} %bitcast.6), calls=%async_computation.1 | async-start | bytes 262144 | tf_op jit(solution)/shard_map/all_to_all | solution.py:109
  195.1 0.1 all-gather.5.cloned.1.call-start
  195.1 0.0 copy-done.4
  195.2 0.1 iota_compare_fusion
  195.2 0.1 multiply_cosine_fusion
  195.3 25.2 %all-to-all-done.1 = bf16[32,8,160]{2,1,0:T(8,128)(2,1)S(1)} async-done(((bf16[32,8,160]{2,1,0:T(8,128)(2,1)}), bf16[32,8,160]{2,1,0:T(8,128)(2,1)S(1)}, u32[]{:S(2)}, u32[]{:S(2)}) %all-to-all-start.1) | async-done | bytes 81952 | tf_op jit(solution)/shard_map/all_to_all | solution.py:109
  220.5 0.2 all_to_all.22
  220.7 0.0 copy-start.1
  220.8 0.1 subtract_convert_fusion.1
  220.9 0.1 subtract_convert_fusion
  221.0 0.1 maximum_bitcast_fusion
  221.1 0.2 fusion.41
  221.3 3.5 fusion.51
  224.8 0.2 fusion.31
  225.1 0.0 copy-done.1
  225.1 0.7 fusion.26
  225.9 0.7 copy.58
  226.5 0.1 all-gather.5.cloned.1.call-update
  226.6 0.0 copy-start.2
  226.6 118.5 %all-gather.5.cloned.1.call-done = bf16[256,4096]{1,0:T(8,128)(2,1)} async-done(((bf16[8,4096]{1,0:T(8,128)(2,1)}), bf16[256,4096]{1,0:T(8,128)(2,1)}) %all-gather.5.cloned.1.call-update) | async-done | bytes 2097168 | tf_op jit(solution)/shard_map/all_gather | solution.py:115
  345.1 2.9 fusion.6
  348.0 1.0 gather_fusion.1
  349.0 0.0 copy-done.2
  349.0 22.1 %collective-permute-start = (bf16[1,256,256]{2,1,0:T(8,128)(2,1)S(1)}, bf16[1,256,256]{2,1,0:T(8,128)(2,1)S(1)}, u32[]{:S(2)}, u32[]{:S(2)}) collective-permute-start(bf16[1,256,256]{2,1,0:T(8,128)(2,1)S(1)} %fusion.36), channel_id=1, source_target_pairs={{0,32},{32,0},{1,33},{33,1},{2,34},{34,2},{3,35},{35,3},{4,36},{36... | collective-permute-start | bytes 393224 | tf_op jit(solution)/shard_map/ppermute | solution.py:30
  371.1 1.0 collective-permute-done
  372.1 0.7 copy.60
  (16 shorter events, 0.2 us)
Async XLA Ops:
  6.5 170.8 %copy-start = (bf16[1,8192,160]{1,2,0:T(8,128)(2,1)S(1)}, bf16[1,8192,160]{1,2,0:T(8,128)(2,1)}, u32[]{:S(2)}) copy-start(bf16[1,8192,160]{1,2,0:T(8,128)(2,1)} %param.10) | copy-start | bytes 7864324
  8.4 54.6 %all-to-all-start = ((f32[32,1,256]{2,1,0:T(1,128)}), f32[32,1,256]{2,1,0:T(1,128)S(1)}, u32[]{:S(2)}, u32[]{:S(2)}) async-start(f32[32,1,256]{2,1,0:T(1,128)} %broadcast_in_dim.23), calls=%async_computation | async-start | bytes 65536 | tf_op jit(solution)/shard_map/all_to_all | solution.py:18
  41.6 135.7 %all-gather.3.cloned.1.call-start = ((), (), s32[]{:S(2)}) async-start(), calls=%async_computation.2 | async-start | bytes 4325376 | tf_op jit(solution)/shard_map/all_gather | solution.py:107
  70.3 5.6 %copy-start.3 = (s32[1,256]{1,0:T(1,128)S(1)}, s32[1,256]{1,0:T(1,128)}, u32[]{:S(2)}) copy-start(s32[1,256]{1,0:T(1,128)} %param.15) | copy-start | bytes 3076
  77.3 117.9 %copy-start.4 = (s32[1,8]{1,0:T(1,128)S(1)}, s32[1,8]{1,0:T(1,128)}, u32[]{:S(2)}) copy-start(s32[1,8]{1,0:T(1,128)} %param.14) | copy-start | bytes 100
  183.0 37.6 %all-to-all-start.1 = ((bf16[32,8,160]{2,1,0:T(8,128)(2,1)}), bf16[32,8,160]{2,1,0:T(8,128)(2,1)S(1)}, u32[]{:S(2)}, u32[]{:S(2)}) async-start(bf16[32,8,160]{2,1,0:T(8,128)(2,1)} %bitcast.6), calls=%async_computation.1 | async-start | bytes 262144 | tf_op jit(solution)/shard_map/all_to_all | solution.py:109
  195.1 150.0 %all-gather.5.cloned.1.call-start = ((), (), s32[]{:S(2)}) async-start(), calls=%async_computation.3 | async-start | bytes 2162688 | tf_op jit(solution)/shard_map/all_gather | solution.py:115
  220.7 4.4 %copy-start.1 = (bf16[8,384,4,128]{3,2,1,0:T(4,128)(2,1)S(1)}, bf16[8,384,4,128]{3,2,1,0:T(4,128)(2,1)}, u32[]{:S(2)}) copy-start(bf16[8,384,4,128]{3,2,1,0:T(4,128)(2,1)} %reshape_squeeze.7) | copy-start | bytes 9437188
  226.6 122.4 %copy-start.2 = (bf16[1,256,256]{2,1,0:T(8,128)(2,1)S(1)}, bf16[1,256,256]{2,1,0:T(8,128)(2,1)}, u32[]{:S(2)}) copy-start(bf16[1,256,256]{2,1,0:T(8,128)(2,1)} %param.8) | copy-start | bytes 393220
  349.0 23.1 %collective-permute-start = (bf16[1,256,256]{2,1,0:T(8,128)(2,1)S(1)}, bf16[1,256,256]{2,1,0:T(8,128)(2,1)S(1)}, u32[]{:S(2)}, u32[]{:S(2)}) collective-permute-start(bf16[1,256,256]{2,1,0:T(8,128)(2,1)S(1)} %fusion.36), channel_id=1, source_target_pairs={{0,32},{32,0},{1,33},{33,1},{2,34},{34,2},{3,35},{35,3},{4,36},{36... | collective-permute-start | bytes 393224 | tf_op jit(solution)/shard_map/ppermute | solution.py:30
Sparse Core Ops, SparseCore 0:
  64.9 112.3 all-gather.2
  226.7 118.3 all-gather.4
where the time goes:
time: 380 us
  waiting for transfers between devices  265 us (70%)
  starting transfers between devices  67.5 us (18%)
  local copies, waits for them, and re-layouts  17.6 us (5%)
  between operations  13.7 us (4%)
  matrix products  11.1 us (3%)
  other arithmetic  4.37 us (1%)
    all_gather x1, waiting for transfers between devices, shards(): lax.all_gather(attended, 'wide', axis=0, tiled=True)  118 us
    all_gather x1, waiting for transfers between devices, shards(): whole = lax.all_gather(normed, 'wide', axis=1, tiled=True)  100 us
    all_to_all x1, starting transfers between devices, copy_for_each(): lax.all_to_all(jnp.broadcast_to(value[None], (count, *value.shape)), axis...  33.2 us
    all_to_all x1, waiting for transfers between devices, shards(): lax.all_to_all(columns[request_at_slot], 'wide', split_axis=0, concat_axi...  25.2 us
    ppermute x1, starting transfers between devices, passed_along(): return lax.ppermute(value, axis, pairs)  22.1 us
    all_to_all x1, waiting for transfers between devices, copy_for_each(): lax.all_to_all(jnp.broadcast_to(value[None], (count, *value.shape)), axis...  20.6 us
    all_to_all x1, starting transfers between devices, shards(): lax.all_to_all(columns[request_at_slot], 'wide', split_axis=0, concat_axi...  12.1 us
  transfers between devices with their start and end apart: 5, of which 5 were waited for; matrix products, arithmetic and copies ran while one was open for 4% of the time, Pallas kernels for 0%

commit v1 on v0

--- a/solution.py
+++ b/solution.py
@@ -104,7 +104,7 @@
         .set(jnp.arange(request_total, dtype=jnp.int32))
     )
     projection = w_qkv[0]
-    whole = lax.all_gather(normed, "wide", axis=1, tiled=True)
+    whole = jnp.concatenate(lax.all_gather(normed, "wide"), axis=1)
     columns = jnp.dot(whole, projection, preferred_element_type=jnp.float32).astype(jnp.bfloat16)
     joined_rows = lax.all_to_all(
         columns[request_at_slot], "wide", split_axis=0, concat_axis=1, tiled=True

time: 380 us -> 373 us (0.982)
  waiting for transfers between devices: 265 us -> 251 us
  local copies, waits for them, and re-layouts: 17.6 us -> 24 us
    all_gather x1, waiting for transfers between devices: 100 us -> 88.9 us  [shards(): whole = jnp.concatenate(lax.all_gather(normed, 'wide'), axis=1)]
    all_gather x0 -> x1, local copies, waits for them, and re-layouts: none -> 6.47 us  [shards(): whole = jnp.concatenate(lax.all_gather(normed, 'wide'), axis=1)]
where the time goes in v1:
time: 373 us; the launch traced here: 372 us
  waiting for transfers between devices  251 us (67%)
  starting transfers between devices  69 us (18%)
  local copies, waits for them, and re-layouts  24 us (6%)
  between operations  13.6 us (4%)
  matrix products  10.5 us (3%)
  other arithmetic  4.37 us (1%)
    all_gather x1, waiting for transfers between devices, shards(): lax.all_gather(attended, 'wide', axis=0, tiled=True)  115 us
    all_gather x1, waiting for transfers between devices, shards(): whole = jnp.concatenate(lax.all_gather(normed, 'wide'), axis=1)  88.9 us
    all_to_all x1, starting transfers between devices, copy_for_each(): lax.all_to_all(jnp.broadcast_to(value[None], (count, *value.shape)), axis...  33.2 us
    all_to_all x1, waiting for transfers between devices, shards(): lax.all_to_all(columns[request_at_slot], 'wide', split_axis=0, concat_axi...  25.2 us
    ppermute x1, starting transfers between devices, passed_along(): return lax.ppermute(value, axis, pairs)  22.1 us
    all_to_all x1, waiting for transfers between devices, copy_for_each(): lax.all_to_all(jnp.broadcast_to(value[None], (count, *value.shape)), axis...  20.6 us
    all_to_all x1, starting transfers between devices, shards(): lax.all_to_all(columns[request_at_slot], 'wide', split_axis=0, concat_axi...  13.6 us
  transfers between devices with their start and end apart: 5, of which 5 were waited for; matrix products, arithmetic and copies ran while one was open for 4% of the time, Pallas kernels for 0%

profile of v1, /device:TPU:37, one launch (start us, length us, event | category | flops | bytes accessed | tf_op | source)
XLA Modules:
  0.0 372.3 jit_solution(12576025373665237875)
XLA Ops:
  6.5 0.0 copy-start
  6.6 1.2 fusion.31
  7.7 0.6 broadcast_in_dim.23
  8.4 33.2 %all-to-all-start = ((f32[32,1,256]{2,1,0:T(1,128)}), f32[32,1,256]{2,1,0:T(1,128)S(1)}, u32[]{:S(2)}, u32[]{:S(2)}) async-start(f32[32,1,256]{2,1,0:T(1,128)} %broadcast_in_dim.23), calls=%async_computation | async-start | bytes 65536 | tf_op jit(solution)/shard_map/all_to_all | solution.py:18
  41.6 0.1 all-gather.3.cloned.1.call-start
  41.6 0.7 mul.190
  42.3 20.6 %all-to-all-done = f32[32,1,256]{2,1,0:T(1,128)S(1)} async-done(((f32[32,1,256]{2,1,0:T(1,128)}), f32[32,1,256]{2,1,0:T(1,128)S(1)}, u32[]{:S(2)}, u32[]{:S(2)}) %all-to-all-start) | async-done | bytes 32800 | tf_op jit(solution)/shard_map/all_to_all | solution.py:18
  63.0 0.1 reduce_sum.28
  63.0 1.7 fusion.33
  64.7 0.1 all-gather.3.cloned.1.call-update
  64.8 5.5 %reshape_squeeze.6 = bf16[8,384,4,128]{3,2,1,0:T(4,128)(2,1)} reshape(bf16[1,8,384,512]{3,2,1,0:T(8,128)(2,1)} %param.12) | data formatting | bytes 6291456 | tf_op jit(solution)/shard_map/reshape;squeeze | solution.py:63
  70.3 0.0 copy-start.3
  70.3 5.5 %reshape_squeeze.7 = bf16[8,384,4,128]{3,2,1,0:T(4,128)(2,1)} reshape(bf16[1,8,384,512]{3,2,1,0:T(8,128)(2,1)} %param.13) | data formatting | bytes 6291456 | tf_op jit(solution)/shard_map/reshape;squeeze | solution.py:64
  75.8 0.0 copy-done.3
  75.8 1.4 scatter_custom_fusion
  77.2 88.9 %all-gather.3.cloned.1.call-done = bf16[32,256,256]{2,1,0:T(8,128)(2,1)} async-done(((bf16[1,256,256]{2,1,0:T(8,128)(2,1)}), bf16[32,256,256]{2,1,0:T(8,128)(2,1)}) %all-gather.3.cloned.1.call-update) | async-done | bytes 4194320 | tf_op jit(solution)/shard_map/all_gather | solution.py:107
  166.1 6.5 %copy.33 = bf16[32,256,256]{1,2,0:T(8,128)(2,1)} copy(bf16[32,256,256]{2,1,0:T(8,128)(2,1)} %all-gather.3.cloned.1.call-done) | data formatting | bytes 8388608 | tf_op jit(solution)/shard_map/all_gather | solution.py:107
  172.5 0.0 copy-done
  172.5 0.0 copy-start.4
  172.5 3.0 fusion.20
  175.6 0.1 copy.34
  175.7 1.8 gather_fusion
  177.5 13.6 %all-to-all-start.1 = ((bf16[32,8,160]{2,1,0:T(8,128)(2,1)}), bf16[32,8,160]{2,1,0:T(8,128)(2,1)S(1)}, u32[]{:S(2)}, u32[]{:S(2)}) async-start(bf16[32,8,160]{2,1,0:T(8,128)(2,1)} %bitcast.7), calls=%async_computation.1 | async-start | bytes 262144 | tf_op jit(solution)/shard_map/all_to_all | solution.py:109
  191.1 0.1 all-gather.5.cloned.1.call-start
  191.2 0.0 copy-done.4
  191.2 0.1 iota_compare_fusion
  191.3 0.1 multiply_cosine_fusion
  191.4 25.2 %all-to-all-done.1 = bf16[32,8,160]{2,1,0:T(8,128)(2,1)S(1)} async-done(((bf16[32,8,160]{2,1,0:T(8,128)(2,1)}), bf16[32,8,160]{2,1,0:T(8,128)(2,1)S(1)}, u32[]{:S(2)}, u32[]{:S(2)}) %all-to-all-start.1) | async-done | bytes 81952 | tf_op jit(solution)/shard_map/all_to_all | solution.py:109
  216.6 0.2 all_to_all.22
  216.8 0.0 copy-start.1
  216.9 0.1 subtract_convert_fusion.1
  216.9 0.1 subtract_convert_fusion
  217.0 0.1 maximum_bitcast_fusion
  217.1 0.2 fusion.39
  217.3 3.5 fusion.49
  220.9 0.2 fusion.29
  221.2 0.0 copy-done.1
  221.2 0.7 fusion.26
  221.9 0.7 copy.67
  222.6 0.1 all-gather.5.cloned.1.call-update
  222.7 0.0 copy-start.2
  222.7 115.1 %all-gather.5.cloned.1.call-done = bf16[256,4096]{1,0:T(8,128)(2,1)} async-done(((bf16[8,4096]{1,0:T(8,128)(2,1)}), bf16[256,4096]{1,0:T(8,128)(2,1)}) %all-gather.5.cloned.1.call-update) | async-done | bytes 2097168 | tf_op jit(solution)/shard_map/all_gather | solution.py:115
  337.7 2.9 fusion.6
  340.7 1.0 gather_fusion.1
  341.6 0.0 copy-done.2
  341.7 22.1 %collective-permute-start = (bf16[1,256,256]{2,1,0:T(8,128)(2,1)S(1)}, bf16[1,256,256]{2,1,0:T(8,128)(2,1)S(1)}, u32[]{:S(2)}, u32[]{:S(2)}) collective-permute-start(bf16[1,256,256]{2,1,0:T(8,128)(2,1)S(1)} %fusion.34), channel_id=1, source_target_pairs={{0,32},{32,0},{1,33},{33,1},{2,34},{34,2},{3,35},{35,3},{4,36},{36... | collective-permute-start | bytes 393224 | tf_op jit(solution)/shard_map/ppermute | solution.py:30
  363.8 1.0 collective-permute-done
  364.8 0.7 copy.69
  (16 shorter events, 0.2 us)
Async XLA Ops:
  6.5 166.0 %copy-start = (bf16[1,8192,160]{1,2,0:T(8,128)(2,1)S(1)}, bf16[1,8192,160]{1,2,0:T(8,128)(2,1)}, u32[]{:S(2)}) copy-start(bf16[1,8192,160]{1,2,0:T(8,128)(2,1)} %param.10) | copy-start | bytes 7864324
  8.4 54.6 %all-to-all-start = ((f32[32,1,256]{2,1,0:T(1,128)}), f32[32,1,256]{2,1,0:T(1,128)S(1)}, u32[]{:S(2)}, u32[]{:S(2)}) async-start(f32[32,1,256]{2,1,0:T(1,128)} %broadcast_in_dim.23), calls=%async_computation | async-start | bytes 65536 | tf_op jit(solution)/shard_map/all_to_all | solution.py:18
  41.6 124.5 %all-gather.3.cloned.1.call-start = ((), (), s32[]{:S(2)}) async-start(), calls=%async_computation.2 | async-start | bytes 4325376 | tf_op jit(solution)/shard_map/all_gather | solution.py:107
  70.3 5.5 %copy-start.3 = (s32[1,256]{1,0:T(1,128)S(1)}, s32[1,256]{1,0:T(1,128)}, u32[]{:S(2)}) copy-start(s32[1,256]{1,0:T(1,128)} %param.15) | copy-start | bytes 3076
  172.5 18.6 %copy-start.4 = (s32[1,8]{1,0:T(1,128)S(1)}, s32[1,8]{1,0:T(1,128)}, u32[]{:S(2)}) copy-start(s32[1,8]{1,0:T(1,128)} %param.14) | copy-start | bytes 100
  177.5 39.1 %all-to-all-start.1 = ((bf16[32,8,160]{2,1,0:T(8,128)(2,1)}), bf16[32,8,160]{2,1,0:T(8,128)(2,1)S(1)}, u32[]{:S(2)}, u32[]{:S(2)}) async-start(bf16[32,8,160]{2,1,0:T(8,128)(2,1)} %bitcast.7), calls=%async_computation.1 | async-start | bytes 262144 | tf_op jit(solution)/shard_map/all_to_all | solution.py:109
  191.1 146.6 %all-gather.5.cloned.1.call-start = ((), (), s32[]{:S(2)}) async-start(), calls=%async_computation.3 | async-start | bytes 2162688 | tf_op jit(solution)/shard_map/all_gather | solution.py:115
  216.8 4.4 %copy-start.1 = (bf16[8,384,4,128]{3,2,1,0:T(4,128)(2,1)S(1)}, bf16[8,384,4,128]{3,2,1,0:T(4,128)(2,1)}, u32[]{:S(2)}) copy-start(bf16[8,384,4,128]{3,2,1,0:T(4,128)(2,1)} %reshape_squeeze.7) | copy-start | bytes 9437188
  222.7 119.0 %copy-start.2 = (bf16[1,256,256]{2,1,0:T(8,128)(2,1)S(1)}, bf16[1,256,256]{2,1,0:T(8,128)(2,1)}, u32[]{:S(2)}) copy-start(bf16[1,256,256]{2,1,0:T(8,128)(2,1)} %param.8) | copy-start | bytes 393220
  341.7 23.1 %collective-permute-start = (bf16[1,256,256]{2,1,0:T(8,128)(2,1)S(1)}, bf16[1,256,256]{2,1,0:T(8,128)(2,1)S(1)}, u32[]{:S(2)}, u32[]{:S(2)}) collective-permute-start(bf16[1,256,256]{2,1,0:T(8,128)(2,1)S(1)} %fusion.34), channel_id=1, source_target_pairs={{0,32},{32,0},{1,33},{33,1},{2,34},{34,2},{3,35},{35,3},{4,36},{36... | collective-permute-start | bytes 393224 | tf_op jit(solution)/shard_map/ppermute | solution.py:30
Sparse Core Ops, SparseCore 0:
  64.9 101.1 all-gather.2
  222.8 114.9 all-gather.4
